TPU v7x, 16 devices: a 4x2x1 block of a 4x4x8 slice. The times are simulated.
16 devices in a mesh: dp: 2 (over y, z), tp: 8 (over x, core).
Axes of the slice: x: 4, y: 2, z: 1, core: 2. Of those that a mesh axis runs over, the one named last changes fastest.
The devices are a block of a 4x4x8 slice.
Arguments:
- hidden: bfloat16 [32, 24, 4096], P('dp'), parts along dimension 0
- tree_mask: int32 [32, 24, 24], P('dp'), parts along dimension 0
- depth: int32 [32, 24], P('dp'), parts along dimension 0
- ctx_len: int32 [32], P('dp'), parts along dimension 0
- block_table: int32 [32, 12], P('dp'), parts along dimension 0
- score_id: int32 [32, 24], P('dp'), parts along dimension 0
- k_cache: bfloat16 [384, 16, 32, 128], P('dp', None, 'tp'), parts along dimension 0
- v_cache: bfloat16 [384, 16, 32, 128], P('dp', None, 'tp'), parts along dimension 0
- attn_norm: bfloat16 [4096], replicated
- w_q: bfloat16 [4096, 4096], P(None, 'tp')
- w_k: bfloat16 [4096, 4096], P(None, 'tp')
- w_v: bfloat16 [4096, 4096], P(None, 'tp')
- w_o: bfloat16 [4096, 4096], P('tp')
- mlp_norm: bfloat16 [4096], replicated
- w_gate: bfloat16 [4096, 11008], P(None, 'tp')
- w_up: bfloat16 [4096, 11008], P(None, 'tp')
- w_down: bfloat16 [11008, 4096], P('tp')
- final_norm: bfloat16 [4096], replicated
- w_lm: bfloat16 [4096, 32000], P(None, 'tp')
Outputs:
- output 1: float32 [32, 24], P('dp'), parts along dimension 0
- output 2: float32 [32, 24], P('dp'), parts along dimension 0
- output 3: bfloat16 [384, 16, 32, 128], P('dp', None, 'tp'), parts along dimension 0
- output 4: bfloat16 [384, 16, 32, 128], P('dp', None, 'tp'), parts along dimension 0
There are 2 independent parts. A program takes and returns all parts, laid end to end along the dimension named above; an argument that names none is the same for every part.
All inputs are finite; a program needn't handle non-finite values.
Results may differ from a plain program's by a relative error of at most 0.00375906.
Values are sent between devices in bfloat16 or wider.
A program may use at most 768 MiB of HBM per device.

v0:
```python
import functools

import jax
import jax.numpy as jnp
import numpy as np
from jax import lax
from jax.experimental import pallas as pl
from jax.experimental.pallas import tpu as pltpu
from jax.sharding import PartitionSpec as P

RMS_EPS = 1e-5
ROPE_THETA = 500000
STEPS = 4
SPAN = 1024
GATE = 512
HEAD = 1024
TILE = 256
VMEM_LIMIT = 66_000_000
HBM = pl.BlockSpec(memory_space=pl.ANY)
VMEM = pl.BlockSpec(memory_space=pltpu.VMEM)
LAST = (((1,), (1,)), ((), ()))
SMEM = pl.BlockSpec(memory_space=pltpu.SMEM)


def norm_rows(wide, gain):
    scale = lax.rsqrt(jnp.mean(wide * wide, axis=-1, keepdims=True) + RMS_EPS)
    return (wide * scale * gain).astype(jnp.bfloat16)


def gain_row(ref):
    wide = ref[...].astype(jnp.float32)
    return jnp.concatenate([wide[i:i + 1, :] for i in range(wide.shape[0])], axis=1)


def column_of(ref, b):
    nodes = ref.shape[1]
    down = lax.broadcasted_iota(jnp.int32, (nodes, nodes), 0)
    across = lax.broadcasted_iota(jnp.int32, (nodes, nodes), 1)
    row = ref[pl.ds(b, 1), :].astype(jnp.float32)
    return jnp.sum(jnp.where(down == across, row, 0.0), axis=-1, keepdims=True)


def attention_kernel(
    dims, ctx_ref, table_ref, depth_ref, freq_ref, hidden_hbm, gain_ref, mask_ref, wq_hbm, wk_hbm, wv_hbm, k_hbm, v_hbm,
    att_ref, k_out, v_out, hid, normed, weights, kc, vc, cosine, sine, gain_buf, head_bias, q_buf, k_buf, v_buf, o_buf, in_sems, out_sems,
):
    requests, nodes, pages, page_rows, heads, head_dim = dims
    rows = requests * nodes
    stack = heads * nodes
    span_rows = pages * page_rows
    half_rows = rows // 2
    f32, bf16, i32 = jnp.float32, jnp.bfloat16, jnp.int32
    copies = []
    for part in range(2):
        piece = pl.ds(part * half_rows, half_rows)
        copies.append(pltpu.make_async_copy(hidden_hbm.at[piece], hid.at[piece], in_sems.at[part]))
    for i, w in enumerate((wq_hbm, wk_hbm, wv_hbm)):
        copies.append(pltpu.make_async_copy(w, weights.at[i], in_sems.at[2 + i]))
    copies.append(pltpu.make_async_copy(k_hbm, kc, in_sems.at[5]))
    copies.append(pltpu.make_async_copy(v_hbm, vc, in_sems.at[6]))
    for copy in copies:
        copy.start()

    gain_buf[...] = gain_row(gain_ref)
    lane = lax.broadcasted_iota(i32, (1, head_dim), 1)
    sign = jnp.where(lane < head_dim // 2, -1.0, 1.0)

    def angle_step(b, _):
        mine = pl.ds(pl.multiple_of(b * nodes, 8), nodes)
        angle = (column_of(depth_ref, b) + ctx_ref[b].astype(f32)) * freq_ref[...]
        cosine[mine, :] = jnp.cos(angle)
        sine[mine, :] = jnp.sin(angle) * sign
        return 0

    lax.fori_loop(0, requests, angle_step, 0)
    span_col = lax.broadcasted_iota(i32, (1, span_rows), 1)
    slot_col = span_col // heads
    stack_row = lax.broadcasted_iota(i32, (stack, 1), 0)
    stack_col = lax.broadcasted_iota(i32, (1, stack), 1)
    head_bias[...] = jnp.where((span_col % heads) == (stack_row // nodes), 0.0, -jnp.inf)

    group = 16
    for part in range(2):
        copies[part].wait()

        def norm_step(i, _, part=part):
            gain = gain_buf[...]
            at = [pl.ds(pl.multiple_of(part * half_rows + (i * 2 + k) * group, group), group) for k in range(2)]
            scales = []
            for p in at:
                wide = hid[p, :].astype(f32)
                scales.append(lax.rsqrt(jnp.mean(wide * wide, axis=-1, keepdims=True) + RMS_EPS))
            for p, scale in zip(at, scales):
                normed[p, :] = (hid[p, :].astype(f32) * scale * gain).astype(bf16)
            return 0

        lax.fori_loop(0, half_rows // group // 2, norm_step, 0)

    width = heads * head_dim
    for i, buf in enumerate((q_buf, k_buf, v_buf)):
        copies[2 + i].wait()

        def project(t, _, i=i, buf=buf):
            cols = pl.ds(pl.multiple_of(t * TILE, TILE), TILE)
            out = jnp.dot(normed[...], weights[i, :, cols], preferred_element_type=f32)
            for h in range(TILE // head_dim):
                one = out[:, h * head_dim:(h + 1) * head_dim]
                if i < 2:
                    one = one * cosine[...] + pltpu.roll(one, head_dim // 2, 1) * sine[...]
                one = one.astype(bf16).astype(f32)
                at = pl.ds(pl.multiple_of(t * TILE + h * head_dim, head_dim), head_dim)
                buf[:, at] = one
            return 0

        lax.fori_loop(0, width // TILE, project, 0)

    copies[5].wait()
    copies[6].wait()
    touched = -(-(nodes - 1) // (page_rows // heads)) + 1
    window = touched * page_rows
    row_id = lax.broadcasted_iota(i32, (window, 1), 0)
    put = (stack_col % nodes) * heads + stack_col // nodes
    expand = ((stack_row % nodes) == lax.broadcasted_iota(i32, (1, nodes), 1)).astype(bf16)
    spread = ((stack_col % nodes) == lax.broadcasted_iota(i32, (nodes, 1), 0)).astype(bf16)
    same_head = (stack_row // nodes) == (stack_col // nodes)
    scale = head_dim ** -0.5

    def attend(b):
        ctx = ctx_ref[b]
        at = [pl.ds(pl.multiple_of(table_ref[b, j] * page_rows, page_rows), page_rows) for j in range(pages)]
        mine = pl.ds(pl.multiple_of(b * nodes, 8), nodes)

        def stacked(buf):
            parts = [buf[mine, h * head_dim:(h + 1) * head_dim] for h in range(heads)]
            return jnp.concatenate(parts, axis=0).astype(bf16)

        query, key, val = stacked(q_buf), stacked(k_buf), stacked(v_buf)
        keys = jnp.concatenate([kc[p, :] for p in at], axis=0)
        vals = jnp.concatenate([vc[p, :] for p in at], axis=0)
        first = jnp.minimum(ctx // (page_rows // heads), pages - touched)
        shift = ctx * heads - first * page_rows
        place = (put + shift == row_id).astype(bf16)
        fresh = (row_id >= shift) & (row_id < shift + stack)
        new = jnp.dot(place, jnp.concatenate([key, val], axis=1), preferred_element_type=f32)
        tree = mask_ref[b].astype(f32).astype(bf16)
        tree = jnp.dot(expand, tree, preferred_element_type=f32).astype(bf16)
        tree = jnp.dot(tree, spread, preferred_element_type=f32)
        score = lax.dot_general(query, keys, LAST, preferred_element_type=f32) * scale
        slot_bias = jnp.where(slot_col < ctx, 0.0, -jnp.inf)
        score = score + (head_bias[...] + slot_bias)
        score_new = lax.dot_general(query, key, LAST, preferred_element_type=f32) * scale
        score_new = jnp.where(same_head & (tree > 0.5), score_new, -jnp.inf)
        top = jnp.maximum(jnp.max(score, axis=-1, keepdims=True), jnp.max(score_new, axis=-1, keepdims=True))
        prob = jnp.exp(score - top)
        prob_new = jnp.exp(score_new - top)
        total = jnp.sum(prob, axis=-1, keepdims=True) + jnp.sum(prob_new, axis=-1, keepdims=True)
        mixed = jnp.dot(prob.astype(bf16), vals, preferred_element_type=f32)
        mixed = (mixed + jnp.dot(prob_new.astype(bf16), val, preferred_element_type=f32)) / total
        stores = []
        for j in range(touched):
            page = pl.ds(pl.multiple_of(table_ref[b, first + j] * page_rows, page_rows), page_rows)
            piece = slice(j * page_rows, (j + 1) * page_rows)
            for c, cache in enumerate((kc, vc)):
                fill = new[piece, c * head_dim:(c + 1) * head_dim]
                old = cache[page, :].astype(f32)
                stores.append((cache, page, jnp.where(fresh[piece], fill, old).astype(bf16)))
        return mine, mixed, stores

    together = 4

    def request_step(i, _):
        done = [attend(i * together + k) for k in range(together)]
        for mine, mixed, stores in done:
            for h in range(heads):
                o_buf[mine, h * head_dim:(h + 1) * head_dim] = mixed[h * nodes:(h + 1) * nodes]
            for cache, page, value in stores:
                cache[page, :] = value
        return 0

    lax.fori_loop(0, requests // together, request_step, 0)
    outs = [pltpu.make_async_copy(kc, k_out, out_sems.at[0]), pltpu.make_async_copy(vc, v_out, out_sems.at[1])]
    for copy in outs:
        copy.start()
    att_ref[...] = o_buf[...].astype(bf16)
    for copy in outs:
        copy.wait()


def attention(hidden, tree_mask, depth, ctx_len, block_table, freq, k_pages, v_pages, attn_norm, w_q, w_k, w_v, dims):
    requests, nodes, pages, page_rows, heads, head_dim = dims
    rows = requests * nodes
    model = hidden.shape[1]
    width = heads * head_dim
    bf16, f32 = jnp.bfloat16, jnp.float32
    scratch = [
        pltpu.VMEM((rows, model), bf16),
        pltpu.VMEM((rows, model), bf16),
        pltpu.VMEM((3, model, width), bf16),
        pltpu.VMEM(k_pages.shape, bf16),
        pltpu.VMEM(v_pages.shape, bf16),
        pltpu.VMEM((rows, head_dim), f32),
        pltpu.VMEM((rows, head_dim), f32),
        pltpu.VMEM((1, model), f32),
        pltpu.VMEM((heads * nodes, pages * page_rows), f32),
    ] + [pltpu.VMEM((rows, width), f32)] * 4 + [pltpu.SemaphoreType.DMA((7,)), pltpu.SemaphoreType.DMA((2,))]
    return pl.pallas_call(
        functools.partial(attention_kernel, dims),
        name="attend",
        out_shape=(
            jax.ShapeDtypeStruct((rows, width), bf16),
            jax.ShapeDtypeStruct(k_pages.shape, bf16),
            jax.ShapeDtypeStruct(v_pages.shape, bf16),
        ),
        in_specs=[SMEM, SMEM, VMEM, VMEM, HBM, VMEM, VMEM, HBM, HBM, HBM, HBM, HBM],
        out_specs=(VMEM, HBM, HBM),
        scratch_shapes=scratch,
        compiler_params=pltpu.CompilerParams(vmem_limit_bytes=VMEM_LIMIT),
    )(ctx_len, block_table, depth, freq, hidden, attn_norm, tree_mask, w_q, w_k, w_v, k_pages, v_pages)


def tail_kernel(
    chips, att_ref, hid_hbm, mlp_gain_ref, fin_gain_ref, score_ref, wo_hbm, wg_hbm, wu_hbm, wd_hbm, lm_hbm,
    top_ref, total_ref, pick_ref, part, sib_in, rel_l, rel_r, in_l, in_r, xg, act, hid_own, run_max, run_sum, run_pick, stats, want_ref, gains,
    send_sems, recv_sems, stat_send, stat_recv, w_sems, lm_sems, hid_sem,
):
    f32, bf16 = jnp.float32, jnp.bfloat16
    rows, model = xg.shape
    ffn = wg_hbm.shape[0]
    vocab = lm_hbm.shape[0]
    members = 2 * chips
    size = rows // members
    quarter = size * chips
    wide = model // STEPS
    sub = wide // 2
    me = lax.axis_index("tp")
    x = me // 2
    core = me % 2
    right = lax.rem(x + 1, chips) * 2 + core
    left = lax.rem(x + chips - 1, chips) * 2 + core
    sib = x * 2 + 1 - core

    barrier = pltpu.get_barrier_semaphore()
    for k in range(1, members):
        pl.semaphore_signal(barrier, inc=1, device_id={"tp": lax.rem(me + k, members)}, device_id_type=pl.DeviceIdType.MESH)

    def first_row(hop):
        return (core * chips + lax.rem(x + hop + chips, chips)) * size

    def block(hop):
        return pl.ds(pl.multiple_of(first_row(hop), 16), size)

    def lanes_of(start, width):
        return pl.ds(start if isinstance(start, int) else pl.multiple_of(start, 128), width)

    def cols(c, part=None):
        if part is None:
            return lanes_of(c * wide, wide)
        return lanes_of(c * wide + part * sub, sub)

    def plan(phase, c, name):
        far = pl.ds(pl.multiple_of((1 - core) * quarter, 16), quarter)
        own, opp, rgt, lft = block(0), block(2), block(1), block(-1)
        both = cols(c)
        c0, c1, here = cols(c, 0), cols(c, 1), lanes_of(c * sub, sub)
        entries = [
            ("pair", part.at[far, both], sib_in.at[:, both], sib),
            ("relay_r", part.at[opp, c0], rel_l.at[:, here], right),
            ("relay_l", part.at[opp, c1], rel_r.at[:, here], left),
            ("direct_r", part.at[rgt, c1], in_l.at[:, c1], right),
            ("direct_l", part.at[lft, c0], in_r.at[:, c0], left),
            ("acc_r", part.at[rgt, c0], in_l.at[:, c0], right),
            ("acc_l", part.at[lft, c1], in_r.at[:, c1], left),
            ("own_r0", xg.at[own, c0], xg.at[own, c0], right),
            ("own_l1", xg.at[own, c1], xg.at[own, c1], left),
            ("own_r1", xg.at[own, c1], xg.at[own, c1], right),
            ("own_l0", xg.at[own, c0], xg.at[own, c0], left),
            ("own_s", xg.at[own, both], xg.at[own, both], sib),
            ("fwd_r", xg.at[lft, c0], xg.at[lft, c0], right),
            ("fwd_l", xg.at[rgt, c1], xg.at[rgt, c1], left),
            ("lft_s", xg.at[lft, both], xg.at[lft, both], sib),
            ("rgt_s", xg.at[rgt, both], xg.at[rgt, both], sib),
            ("opp_s", xg.at[opp, both], xg.at[opp, both], sib),
        ]
        i = [entry[0] for entry in entries].index(name)
        _, src, dst, to = entries[i]
        return pltpu.make_async_remote_copy(
            src_ref=src, dst_ref=dst, send_sem=send_sems.at[phase, c, i], recv_sem=recv_sems.at[phase, c, i],
            device_id={"tp": to}, device_id_type=pl.DeviceIdType.MESH,
        )

    reduce_names = ("pair", "relay_r", "relay_l", "direct_r", "direct_l", "acc_r", "acc_l")
    own_names = ("own_r0", "own_l1", "own_r1", "own_l0", "own_s")
    other_names = ("fwd_r", "fwd_l", "lft_s", "rgt_s", "opp_s")
    steps = range(STEPS)

    def pair_sum(phase, c):
        both = cols(c)
        plan(phase, c, "pair").wait_recv()

        def add(i, _):
            there = pl.ds(pl.multiple_of(core * quarter + i * 32, 16), 32)
            here = pl.ds(pl.multiple_of(i * 32, 32), 32)
            part[there, both] = (part[there, both].astype(f32) + sib_in[here, both].astype(f32)).astype(bf16)
            return 0

        lax.fori_loop(0, quarter // 32, add, 0)
        for name in ("relay_r", "relay_l", "direct_r", "direct_l"):
            plan(phase, c, name).start()

    def accumulate(phase, c):
        here = lanes_of(c * sub, sub)
        for name, hop, which, buf in (("r", 1, 0, rel_l), ("l", -1, 1, rel_r)):
            plan(phase, c, f"relay_{name}").wait_recv()
            at = block(hop)
            part[at, cols(c, which)] = (part[at, cols(c, which)].astype(f32) + buf[:, here].astype(f32)).astype(bf16)
            plan(phase, c, f"acc_{name}").start()

    def own_send(phase, c):
        for name in own_names:
            plan(phase, c, name).start()

    def finish(phase):
        squares = 0.0
        for c in steps:
            both = cols(c)
            for name in ("direct_r", "direct_l", "acc_r", "acc_l"):
                plan(phase, c, name).wait_recv()
            total = part[block(0), both].astype(f32) + in_l[:, both].astype(f32) + in_r[:, both].astype(f32)
            residual = (hid_own[:, both].astype(f32) + total.astype(bf16).astype(f32)).astype(bf16)
            hid_own[:, both] = residual
            full = residual.astype(f32)
            squares = squares + jnp.sum(full * full, axis=-1, keepdims=True)
        scale = lax.rsqrt(squares * (1.0 / model) + RMS_EPS)
        for c in steps:
            both = cols(c)
            xg[block(0), both] = (hid_own[:, both].astype(f32) * scale * gains[phase:phase + 1, both]).astype(bf16)
            if c < 2:
                own_send(phase, c)

    def forward(phase, c, more=True):
        plan(phase, c, "own_r0").wait_recv()
        plan(phase, c, "fwd_r").start()
        plan(phase, c, "own_l1").wait_recv()
        plan(phase, c, "fwd_l").start()
        if more:
            own_send(phase, c + 2)

    def share(phase, c):
        plan(phase, c, "own_r1").wait_recv()
        plan(phase, c, "lft_s").start()
        plan(phase, c, "own_l0").wait_recv()
        plan(phase, c, "rgt_s").start()
        plan(phase, c, "fwd_r").wait_recv()
        plan(phase, c, "fwd_l").wait_recv()
        plan(phase, c, "opp_s").start()

    def ready(phase, c):
        for name in ("own_s", "lft_s", "rgt_s", "opp_s"):
            plan(phase, c, name).wait_recv()

    def drain(phase):
        def one(c, _):
            for name in reduce_names + own_names + other_names:
                plan(phase, c, name).wait_send()
            return 0

        lax.fori_loop(0, STEPS, one, 0)

    def reduce(phase, lhs_ref, w_ref):
        def step(c, _):
            @pl.when(c < STEPS)
            def _():
                part[:, cols(c)] = jnp.dot(lhs_ref[...], w_ref[:, cols(c)], preferred_element_type=f32).astype(bf16)
                plan(phase, c, "pair").start()

            @pl.when((c >= 1) & (c <= STEPS))
            def _():
                pair_sum(phase, c - 1)

            @pl.when(c >= 3)
            def _():
                accumulate(phase, c - 3)

            return 0

        lax.fori_loop(0, STEPS + 3, step, 0)
        finish(phase)

    def gather(phase, compute, loads):
        forward(phase, 0)
        forward(phase, 1)
        share(phase, 0)
        ready(phase, 0)
        forward(phase, 2, False)
        for load in loads:
            load.wait()

        def step(c, _):
            compute(cols(c), False, 0)
            share(phase, c + 1)

            @pl.when(c == 0)
            def _():
                forward(phase, 3, False)

            compute(cols(c), False, 1)

            @pl.when(c == 1)
            def _():
                share(phase, 3)

            @pl.when(c == 0)
            def _():
                ready(phase, 1)

            return 0

        lax.fori_loop(0, 2, step, 0)
        ready(phase, 2)
        ready(phase, 3)
        compute(pl.ds(2 * wide, 2 * wide), True, None)

    def layer(wo, wg, wu, wd, gate_acc, up_acc):
        loads = [
            pltpu.make_async_copy(src, dst, w_sems.at[i])
            for i, (src, dst) in enumerate(((wo_hbm, wo), (wg_hbm, wg), (wu_hbm, wu), (wd_hbm, wd)))
        ]
        loads[0].start()
        own_rows = pltpu.make_async_copy(hid_hbm.at[block(0), :], hid_own, hid_sem.at[0])
        own_rows.start()
        gains[0:1, :] = gain_row(mlp_gain_ref)
        gains[1:2, :] = gain_row(fin_gain_ref)

        def want_step(b, _):
            nodes = score_ref.shape[1]
            column = column_of(score_ref, b).astype(jnp.int32)
            want_ref[pl.ds(pl.multiple_of(b * nodes, 8), nodes), :] = jnp.broadcast_to(column, (nodes, 128))
            return 0

        lax.fori_loop(0, score_ref.shape[0], want_step, 0)
        own_rows.wait()
        loads[0].wait()
        for load in loads[1:]:
            load.start()
        gate_acc[...] = jnp.zeros(gate_acc.shape, f32)
        up_acc[...] = jnp.zeros(up_acc.shape, f32)
        pl.semaphore_wait(barrier, members - 1)
        reduce(0, att_ref, wo)

        def gated(span, is_last, half):
            def close(start, width):
                at = pl.ds(start, width)
                gate = gate_acc[:, at]
                act[:, at] = (gate * jax.nn.sigmoid(gate) * up_acc[:, at]).astype(bf16)

            def tile(start, width):
                at = pl.ds(start, width)
                for w, acc in ((wg, gate_acc), (wu, up_acc)):
                    acc[:, at] += lax.dot_general(xg[:, span], w[at, span], LAST, preferred_element_type=f32)

            def step(t, _):
                tile(pl.multiple_of(t * GATE, GATE), GATE)
                return 0

            def last_step(t, _):
                tile(pl.multiple_of(t * GATE, GATE), GATE)
                close(pl.multiple_of((t - 1) * GATE, GATE), GATE)
                return 0

            full = ffn // GATE
            if is_last:
                tile(0, GATE)
                lax.fori_loop(1, full, last_step, 0)
                tile(full * GATE, ffn - full * GATE)
                close((full - 1) * GATE, GATE)
                close(full * GATE, ffn - full * GATE)
            elif half == 0:
                lax.fori_loop(0, full, step, 0)
            else:
                tile(full * GATE, ffn - full * GATE)

        gather(0, gated, loads[1:3])
        drain(0)
        loads[3].wait()
        reduce(1, act, wd)

    pl.run_scoped(
        layer,
        pltpu.VMEM(wo_hbm.shape, bf16), pltpu.VMEM((ffn, model), bf16), pltpu.VMEM((ffn, model), bf16), pltpu.VMEM((ffn, model), bf16),
        pltpu.VMEM((rows, ffn), f32), pltpu.VMEM((rows, ffn), f32),
    )

    pieces = 5
    lanes = 128

    def head(lm, acc):
        loads = []
        step_rows = vocab // pieces
        for i in range(pieces):
            piece = pl.ds(i * step_rows, step_rows)
            loads.append(pltpu.make_async_copy(lm_hbm.at[piece, :], lm.at[piece, :], lm_sems.at[i]))
            loads[-1].start()
        run_max[...] = jnp.full(run_max.shape, -jnp.inf, f32)
        run_sum[...] = jnp.zeros(run_sum.shape, f32)
        run_pick[...] = jnp.zeros(run_pick.shape, f32)
        full = vocab // HEAD
        rest = vocab % HEAD
        whole = rest // lanes * lanes

        def fold(base, width):
            parts = [acc[:, pl.ds(base + i * lanes, lanes)] for i in range(width // lanes)]
            old = run_max[...]
            new = functools.reduce(jnp.maximum, parts, old)
            lane = lax.broadcasted_iota(jnp.int32, (1, lanes), 1) + base + me * vocab
            want = want_ref[...]
            total = run_sum[...] * jnp.exp(old - new)
            pick = run_pick[...]
            for i, one in enumerate(parts):
                total = total + jnp.exp(one - new)
                pick = pick + jnp.where(lane + i * lanes == want, one, 0.0)
            run_max[...] = new
            run_sum[...] = total
            run_pick[...] = pick

        def logits(span, is_last, half):
            def tile(base, width):
                at = pl.ds(base, width)
                acc[:, at] += lax.dot_general(xg[:, span], lm[at, span], LAST, preferred_element_type=f32)

            def step(t, _):
                tile(pl.multiple_of(t * HEAD, HEAD), HEAD)
                if is_last:
                    fold(pl.multiple_of((t - 1) * HEAD, HEAD), HEAD)
                return 0

            cut = (full + 1) // 2
            if is_last:
                tile(0, HEAD)
                lax.fori_loop(1, full, step, 0)
                tile(full * HEAD, rest)
                fold((full - 1) * HEAD, HEAD)
            elif half == 0:
                lax.fori_loop(0, cut, step, 0)
            else:
                lax.fori_loop(cut, full, step, 0)
                tile(full * HEAD, rest)

        acc[...] = jnp.zeros(acc.shape, f32)
        gather(1, logits, loads)
        fold(full * HEAD, whole)
        end = acc[:, full * HEAD + whole:vocab]
        top = jnp.maximum(jnp.max(run_max[...], axis=-1, keepdims=True), jnp.max(end, axis=-1, keepdims=True))
        total = jnp.sum(run_sum[...] * jnp.exp(run_max[...] - top), axis=-1, keepdims=True)
        total = total + jnp.sum(jnp.exp(end - top), axis=-1, keepdims=True)
        lane = lax.broadcasted_iota(jnp.int32, (1, rest - whole), 1) + (full * HEAD + whole) + me * vocab
        pick = jnp.sum(run_pick[...], axis=-1, keepdims=True)
        pick = pick + jnp.sum(jnp.where(lane == want_ref[:, 0:1], end, 0.0), axis=-1, keepdims=True)
        place = lax.broadcasted_iota(jnp.int32, (1, lanes), 1)
        packed = jnp.where(place == 0, top, jnp.where(place == 1, total, pick))
        stats[me] = packed.T[0:8, :]

    pl.run_scoped(head, pltpu.VMEM((vocab, model), bf16), pltpu.VMEM((rows, vocab), f32))

    sends = []
    for k in range(1, members):
        to = lax.rem(me + k, members)
        sends.append(pltpu.make_async_remote_copy(
            src_ref=stats.at[me], dst_ref=stats.at[me], send_sem=stat_send.at[k - 1], recv_sem=stat_recv.at[k - 1],
            device_id={"tp": to}, device_id_type=pl.DeviceIdType.MESH,
        ))
        sends[-1].start()
    drain(1)
    for copy in sends:
        copy.wait()
    every = [stats[i] for i in range(members)]
    top = functools.reduce(jnp.maximum, [e[0:1, :] for e in every])
    total = functools.reduce(jnp.add, [e[1:2, :] * jnp.exp(e[0:1, :] - top) for e in every])
    pick = functools.reduce(jnp.add, [e[2:3, :] for e in every])
    requests, nodes = score_ref.shape
    for b in range(requests):
        for ref, row in ((top_ref, top), (total_ref, total), (pick_ref, pick)):
            ref[b:b + 1, :] = row[:, b * nodes:(b + 1) * nodes]


def tail(attended, hidden, mlp_norm, final_norm, score_id, w_o, w_gate, w_up, w_down, w_lm, chips):
    rows, model = hidden.shape
    ffn = w_gate.shape[0]
    members = 2 * chips
    bf16, f32 = jnp.bfloat16, jnp.float32
    own = rows // members
    scratch = [
        pltpu.VMEM((rows, model), bf16),
        pltpu.VMEM((rows // 2, model), bf16),
        pltpu.VMEM((own, model // 2), bf16),
        pltpu.VMEM((own, model // 2), bf16),
        pltpu.VMEM((own, model), bf16),
        pltpu.VMEM((own, model), bf16),
        pltpu.VMEM((rows, model), bf16),
        pltpu.VMEM((rows, ffn), bf16),
        pltpu.VMEM((own, model), bf16),
        pltpu.VMEM((rows, 128), f32),
        pltpu.VMEM((rows, 128), f32),
        pltpu.VMEM((rows, 128), f32),
        pltpu.VMEM((members, 8, rows), f32),
        pltpu.VMEM((rows, 128), jnp.int32),
        pltpu.VMEM((2, model), f32),
        pltpu.SemaphoreType.DMA((2, STEPS, 17)),
        pltpu.SemaphoreType.DMA((2, STEPS, 17)),
        pltpu.SemaphoreType.DMA((members - 1,)),
        pltpu.SemaphoreType.DMA((members - 1,)),
        pltpu.SemaphoreType.DMA((4,)),
        pltpu.SemaphoreType.DMA((5,)),
        pltpu.SemaphoreType.DMA((1,)),
    ]
    return pl.pallas_call(
        functools.partial(tail_kernel, chips),
        name="tail",
        out_shape=(jax.ShapeDtypeStruct(score_id.shape, f32),) * 3,
        in_specs=[VMEM, HBM, VMEM, VMEM, VMEM, HBM, HBM, HBM, HBM, HBM],
        out_specs=(VMEM, VMEM, VMEM),
        scratch_shapes=scratch,
        compiler_params=pltpu.CompilerParams(vmem_limit_bytes=VMEM_LIMIT, collective_id=0, has_side_effects=True),
    )(attended, hidden, mlp_norm, final_norm, score_id, w_o, w_gate, w_up, w_down, w_lm)


def solution(mesh):
    chips = mesh.shape["tp"] // 2

    def group_step(hidden, tree_mask, depth, ctx_len, block_table, score_id, k_cache, v_cache, attn_norm, w_q, w_k, w_v, w_o, mlp_norm, w_gate, w_up, w_down, final_norm, w_lm):
        requests, nodes, model = hidden.shape
        blocks, page_size, heads, head_dim = k_cache.shape
        dims = (requests, nodes, block_table.shape[1], page_size * heads, heads, head_dim)
        rows = requests * nodes
        flat = hidden.reshape(rows, model)
        half = head_dim // 2
        inv_freq = 1.0 / (ROPE_THETA ** (jnp.arange(half, dtype=jnp.float32) * (2.0 / head_dim)))
        freq = jnp.concatenate([inv_freq, inv_freq])[None, :]
        pages = (blocks * page_size * heads, head_dim)
        attended, k_out, v_out = attention(
            flat, tree_mask, depth, ctx_len, block_table, freq, k_cache.reshape(pages), v_cache.reshape(pages),
            attn_norm.reshape(model // 128, 128), w_q, w_k, w_v, dims,
        )
        top, total, pick = tail(
            attended, flat, mlp_norm.reshape(model // 128, 128), final_norm.reshape(model // 128, 128), score_id,
            w_o, w_gate.T, w_up.T, w_down, w_lm.T, chips,
        )
        log_norm = top + jnp.log(total)
        return log_norm, pick - log_norm, k_out.reshape(k_cache.shape), v_out.reshape(v_cache.shape)

    request_spec = P("dp", None, None)
    node_spec = P("dp", None)
    cache_spec = P("dp", None, "tp", None)
    shared_spec = P(None)
    column_spec = P(None, "tp")
    row_spec = P("tp", None)
    in_specs = (request_spec, request_spec, node_spec, P("dp"), node_spec, node_spec, cache_spec, cache_spec, shared_spec, column_spec, column_spec, column_spec, row_spec, shared_spec, column_spec, column_spec, row_spec, shared_spec, column_spec)
    out_specs = (node_spec, node_spec, cache_spec, cache_spec)
    return jax.shard_map(group_step, mesh=mesh, in_specs=in_specs, out_specs=out_specs, check_vma=False)
```

profile of v0, /device:TPU:113, one launch (start us, length us, event | category | flops | bytes accessed | tf_op | source)
XLA Modules:
  0.0 128.8 jit_solution(11920174979981397435)
XLA Ops:
  0.6 0.6 maximum_bitcast_fusion.freq_ref
  1.2 23.5 %attend.1 = (bf16[384,512]{1,0:T(8,128)(2,1)}, bf16[12288,128]{1,0:T(8,128)(2,1)}, bf16[12288,128]{1,0:T(8,128)(2,1)}) custom-call(s32[16]{0:T(128)} %ctx_ref.1, s32[16,12]{1,0:T(8,128)} %table_ref.1, s32[16,24]{1,0:T(8,128)} %depth_ref.1, f32[1,128]{1,0:T(1,128)} %maximum_bitcast_fusion.freq_ref, bf16[384,4096]{1,0:T(8,128)(2,1)} %bitcast.14, ...), custom_call_target="tpu_custom_call" | custom-call | tf_op jit(solution)/shard_map/attend/pallas_call | solution.py:206
  24.7 102.7 %tail.1 = (f32[16,24]{1,0:T(8,128)}, f32[16,24]{1,0:T(8,128)}, f32[16,24]{1,0:T(8,128)}) custom-call(bf16[384,512]{1,0:T(8,128)(2,1)} %get-tuple-element.10.att_ref, bf16[384,4096]{1,0:T(8,128)(2,1)} %bitcast.15, bf16[32,128]{1,0:T(8,128)(2,1)} %bitcast.21, bf16[32,128]{1,0:T(8,128)(2,1)} %bitcast.22, s32[16,24]{1,0:T(8,128)} %score_ref.1, ...), custom_call_target="tpu_custom_call" | custom-call | tf_op jit(solution)/shard_map/tail/pallas_call | solution.py:615
  127.4 1.3 %fusion = (f32[16,24]{1,0:T(8,128)}, f32[16,24]{1,0:T(8,128)}) fusion(f32[16,24]{1,0:T(8,128)} %get-tuple-element.13, f32[16,24]{1,0:T(8,128)} %get-tuple-element.11, f32[16,24]{1,0:T(8,128)} %get-tuple-element.12), kind=kLoop, calls=%fused_computation.3 | loop fusion | flops 768 | bytes 7680 | tf_op jit(solution)/shard_map/sub | solution.py:648
  (1 shorter events, 0.0 us)
where the time goes:
time: 129 us
  Pallas kernels  126 us (98%)
  other arithmetic  1.94 us (2%)
    pallas_call x1, Pallas kernels, tail(): pl.pallas_call(functools.partial(tail_kernel, chips), name='tail', out_sh...  103 us
    pallas_call x1, Pallas kernels, attention(): pl.pallas_call(functools.partial(attention_kernel, dims), name='attend',...  23.5 us

commit v1 on v0

--- a/solution.py
+++ b/solution.py
@@ -32,6 +32,10 @@
     return jnp.concatenate([wide[i:i + 1, :] for i in range(wide.shape[0])], axis=1)
 
 
+def window_pages(nodes, page_size):
+    return -(-(nodes - 1) // page_size) + 1
+
+
 def column_of(ref, b):
     nodes = ref.shape[1]
     down = lax.broadcasted_iota(jnp.int32, (nodes, nodes), 0)
@@ -42,7 +46,7 @@
 
 def attention_kernel(
     dims, ctx_ref, table_ref, depth_ref, freq_ref, hidden_hbm, gain_ref, mask_ref, wq_hbm, wk_hbm, wv_hbm, k_hbm, v_hbm,
-    att_ref, k_out, v_out, hid, normed, weights, kc, vc, cosine, sine, gain_buf, head_bias, q_buf, k_buf, v_buf, o_buf, in_sems, out_sems,
+    att_ref, k_out, v_out, hid, normed, weights, kc, vc, cosine, sine, gain_buf, head_bias, q_buf, k_buf, v_buf, o_buf, renewed, in_sems, out_sems,
 ):
     requests, nodes, pages, page_rows, heads, head_dim = dims
     rows = requests * nodes
@@ -58,7 +62,7 @@
         copies.append(pltpu.make_async_copy(w, weights.at[i], in_sems.at[2 + i]))
     copies.append(pltpu.make_async_copy(k_hbm, kc, in_sems.at[5]))
     copies.append(pltpu.make_async_copy(v_hbm, vc, in_sems.at[6]))
-    for copy in copies:
+    for copy in copies[:3]:
         copy.start()
 
     gain_buf[...] = gain_row(gain_ref)
@@ -73,6 +77,8 @@
         return 0
 
     lax.fori_loop(0, requests, angle_step, 0)
+    for copy in copies[3:]:
+        copy.start()
     span_col = lax.broadcasted_iota(i32, (1, span_rows), 1)
     slot_col = span_col // heads
     stack_row = lax.broadcasted_iota(i32, (stack, 1), 0)
@@ -96,6 +102,7 @@
 
         lax.fori_loop(0, half_rows // group // 2, norm_step, 0)
 
+    flush = [pltpu.make_async_copy(cache, out, out_sems.at[k]) for k, (cache, out) in enumerate(((kc, k_out), (vc, v_out)))]
     width = heads * head_dim
     for i, buf in enumerate((q_buf, k_buf, v_buf)):
         copies[2 + i].wait()
@@ -113,10 +120,12 @@
             return 0
 
         lax.fori_loop(0, width // TILE, project, 0)
-
-    copies[5].wait()
-    copies[6].wait()
-    touched = -(-(nodes - 1) // (page_rows // heads)) + 1
+        if i == 1:
+            for k, whole in enumerate(flush):
+                copies[5 + k].wait()
+                whole.start()
+
+    touched = window_pages(nodes, page_rows // heads)
     window = touched * page_rows
     row_id = lax.broadcasted_iota(i32, (window, 1), 0)
     put = (stack_col % nodes) * heads + stack_col // nodes
@@ -163,27 +172,32 @@
             for c, cache in enumerate((kc, vc)):
                 fill = new[piece, c * head_dim:(c + 1) * head_dim]
                 old = cache[page, :].astype(f32)
-                stores.append((cache, page, jnp.where(fresh[piece], fill, old).astype(bf16)))
+                stores.append((c, j, page, jnp.where(fresh[piece], fill, old).astype(bf16)))
         return mine, mixed, stores
 
     together = 4
+    for whole in flush:
+        whole.wait()
 
     def request_step(i, _):
         done = [attend(i * together + k) for k in range(together)]
-        for mine, mixed, stores in done:
+        for k, (mine, mixed, stores) in enumerate(done):
             for h in range(heads):
                 o_buf[mine, h * head_dim:(h + 1) * head_dim] = mixed[h * nodes:(h + 1) * nodes]
-            for cache, page, value in stores:
-                cache[page, :] = value
+            for c, j, page, value in stores:
+                slot = pl.ds(pl.multiple_of((i * together + k) * window + j * page_rows, page_rows), page_rows)
+                renewed[c, slot, :] = value
+        for k, (mine, mixed, stores) in enumerate(done):
+            for c, j, page, value in stores:
+                slot = pl.ds(pl.multiple_of((i * together + k) * window + j * page_rows, page_rows), page_rows)
+                out = (k_out, v_out)[c]
+                pltpu.make_async_copy(renewed.at[c, slot, :], out.at[page, :], out_sems.at[2 + c]).start()
         return 0
 
     lax.fori_loop(0, requests // together, request_step, 0)
-    outs = [pltpu.make_async_copy(kc, k_out, out_sems.at[0]), pltpu.make_async_copy(vc, v_out, out_sems.at[1])]
-    for copy in outs:
-        copy.start()
     att_ref[...] = o_buf[...].astype(bf16)
-    for copy in outs:
-        copy.wait()
+    for c, out in enumerate((k_out, v_out)):
+        pltpu.make_async_copy(renewed.at[c], out.at[pl.ds(0, requests * window), :], out_sems.at[2 + c]).wait()
 
 
 def attention(hidden, tree_mask, depth, ctx_len, block_table, freq, k_pages, v_pages, attn_norm, w_q, w_k, w_v, dims):
@@ -192,6 +206,7 @@
     model = hidden.shape[1]
     width = heads * head_dim
     bf16, f32 = jnp.bfloat16, jnp.float32
+    window = window_pages(nodes, page_rows // heads) * page_rows
     scratch = [
         pltpu.VMEM((rows, model), bf16),
         pltpu.VMEM((rows, model), bf16),
@@ -202,7 +217,7 @@
         pltpu.VMEM((rows, head_dim), f32),
         pltpu.VMEM((1, model), f32),
         pltpu.VMEM((heads * nodes, pages * page_rows), f32),
-    ] + [pltpu.VMEM((rows, width), f32)] * 4 + [pltpu.SemaphoreType.DMA((7,)), pltpu.SemaphoreType.DMA((2,))]
+    ] + [pltpu.VMEM((rows, width), f32)] * 4 + [pltpu.VMEM((2, requests * window, head_dim), bf16), pltpu.SemaphoreType.DMA((7,)), pltpu.SemaphoreType.DMA((4,))]
     return pl.pallas_call(
         functools.partial(attention_kernel, dims),
         name="attend",
@@ -221,7 +236,7 @@
 def tail_kernel(
     chips, att_ref, hid_hbm, mlp_gain_ref, fin_gain_ref, score_ref, wo_hbm, wg_hbm, wu_hbm, wd_hbm, lm_hbm,
     top_ref, total_ref, pick_ref, part, sib_in, rel_l, rel_r, in_l, in_r, xg, act, hid_own, run_max, run_sum, run_pick, stats, want_ref, gains,
-    send_sems, recv_sems, stat_send, stat_recv, w_sems, lm_sems, hid_sem,
+    send_sems, recv_sems, stat_send, stat_recv, w_sems, wo_sems, lm_sems, hid_sem,
 ):
     f32, bf16 = jnp.float32, jnp.bfloat16
     rows, model = xg.shape
@@ -366,10 +381,11 @@
 
         lax.fori_loop(0, STEPS, one, 0)
 
-    def reduce(phase, lhs_ref, w_ref):
+    def reduce(phase, lhs_ref, w_ref, before, filler):
         def step(c, _):
             @pl.when(c < STEPS)
             def _():
+                before(c)
                 part[:, cols(c)] = jnp.dot(lhs_ref[...], w_ref[:, cols(c)], preferred_element_type=f32).astype(bf16)
                 plan(phase, c, "pair").start()
 
@@ -384,6 +400,7 @@
             return 0
 
         lax.fori_loop(0, STEPS + 3, step, 0)
+        filler()
         finish(phase)
 
     def gather(phase, compute, loads):
@@ -423,29 +440,33 @@
     def layer(wo, wg, wu, wd, gate_acc, up_acc):
         loads = [
             pltpu.make_async_copy(src, dst, w_sems.at[i])
-            for i, (src, dst) in enumerate(((wo_hbm, wo), (wg_hbm, wg), (wu_hbm, wu), (wd_hbm, wd)))
+            for i, (src, dst) in enumerate(((wg_hbm, wg), (wu_hbm, wu), (wd_hbm, wd)))
         ]
-        loads[0].start()
+        def wo_piece(c):
+            return pltpu.make_async_copy(wo_hbm.at[:, cols(c)], wo.at[:, cols(c)], wo_sems.at[c])
+
+        for c in steps:
+            wo_piece(c).start()
         own_rows = pltpu.make_async_copy(hid_hbm.at[block(0), :], hid_own, hid_sem.at[0])
         own_rows.start()
-        gains[0:1, :] = gain_row(mlp_gain_ref)
-        gains[1:2, :] = gain_row(fin_gain_ref)
-
-        def want_step(b, _):
-            nodes = score_ref.shape[1]
-            column = column_of(score_ref, b).astype(jnp.int32)
-            want_ref[pl.ds(pl.multiple_of(b * nodes, 8), nodes), :] = jnp.broadcast_to(column, (nodes, 128))
-            return 0
-
-        lax.fori_loop(0, score_ref.shape[0], want_step, 0)
-        own_rows.wait()
-        loads[0].wait()
-        for load in loads[1:]:
-            load.start()
-        gate_acc[...] = jnp.zeros(gate_acc.shape, f32)
-        up_acc[...] = jnp.zeros(up_acc.shape, f32)
+
+        def before(c):
+            wo_piece(c).wait()
+
+            @pl.when(c == STEPS - 1)
+            def _():
+                for load in loads:
+                    load.start()
+
+        def filler():
+            gains[0:1, :] = gain_row(mlp_gain_ref)
+            gains[1:2, :] = gain_row(fin_gain_ref)
+            gate_acc[...] = jnp.zeros(gate_acc.shape, f32)
+            up_acc[...] = jnp.zeros(up_acc.shape, f32)
+            own_rows.wait()
+
         pl.semaphore_wait(barrier, members - 1)
-        reduce(0, att_ref, wo)
+        reduce(0, att_ref, wo, before, filler)
 
         def gated(span, is_last, half):
             def close(start, width):
@@ -462,27 +483,23 @@
                 tile(pl.multiple_of(t * GATE, GATE), GATE)
                 return 0
 
-            def last_step(t, _):
-                tile(pl.multiple_of(t * GATE, GATE), GATE)
-                close(pl.multiple_of((t - 1) * GATE, GATE), GATE)
-                return 0
-
             full = ffn // GATE
             if is_last:
-                tile(0, GATE)
-                lax.fori_loop(1, full, last_step, 0)
-                tile(full * GATE, ffn - full * GATE)
-                close((full - 1) * GATE, GATE)
-                close(full * GATE, ffn - full * GATE)
+                pieces = [(t * GATE, min(GATE, ffn - t * GATE)) for t in range(-(-ffn // GATE))]
+                tile(*pieces[0])
+                for t in range(1, len(pieces)):
+                    close(*pieces[t - 1])
+                    tile(*pieces[t])
+                close(*pieces[-1])
             elif half == 0:
                 lax.fori_loop(0, full, step, 0)
             else:
                 tile(full * GATE, ffn - full * GATE)
 
-        gather(0, gated, loads[1:3])
+        gather(0, gated, loads[:2])
         drain(0)
-        loads[3].wait()
-        reduce(1, act, wd)
+        loads[2].wait()
+        reduce(1, act, wd, lambda c: None, lambda: None)
 
     pl.run_scoped(
         layer,
@@ -500,6 +517,14 @@
             piece = pl.ds(i * step_rows, step_rows)
             loads.append(pltpu.make_async_copy(lm_hbm.at[piece, :], lm.at[piece, :], lm_sems.at[i]))
             loads[-1].start()
+
+        def want_step(b, _):
+            nodes = score_ref.shape[1]
+            column = column_of(score_ref, b).astype(jnp.int32)
+            want_ref[pl.ds(pl.multiple_of(b * nodes, 8), nodes), :] = jnp.broadcast_to(column, (nodes, 128))
+            return 0
+
+        lax.fori_loop(0, score_ref.shape[0], want_step, 0)
         run_max[...] = jnp.full(run_max.shape, -jnp.inf, f32)
         run_sum[...] = jnp.zeros(run_sum.shape, f32)
         run_pick[...] = jnp.zeros(run_pick.shape, f32)
@@ -529,16 +554,16 @@
 
             def step(t, _):
                 tile(pl.multiple_of(t * HEAD, HEAD), HEAD)
-                if is_last:
-                    fold(pl.multiple_of((t - 1) * HEAD, HEAD), HEAD)
                 return 0
 
             cut = (full + 1) // 2
             if is_last:
-                tile(0, HEAD)
-                lax.fori_loop(1, full, step, 0)
+                for t in range(full):
+                    tile(t * HEAD, HEAD)
+                    if t > 0:
+                        fold((t - 1) * HEAD, HEAD)
+                fold((full - 1) * HEAD, HEAD)
                 tile(full * HEAD, rest)
-                fold((full - 1) * HEAD, HEAD)
             elif half == 0:
                 lax.fori_loop(0, cut, step, 0)
             else:
@@ -608,7 +633,8 @@
         pltpu.SemaphoreType.DMA((2, STEPS, 17)),
         pltpu.SemaphoreType.DMA((members - 1,)),
         pltpu.SemaphoreType.DMA((members - 1,)),
-        pltpu.SemaphoreType.DMA((4,)),
+        pltpu.SemaphoreType.DMA((3,)),
+        pltpu.SemaphoreType.DMA((STEPS,)),
         pltpu.SemaphoreType.DMA((5,)),
         pltpu.SemaphoreType.DMA((1,)),
     ]
@@ -632,9 +658,8 @@
         dims = (requests, nodes, block_table.shape[1], page_size * heads, heads, head_dim)
         rows = requests * nodes
         flat = hidden.reshape(rows, model)
-        half = head_dim // 2
-        inv_freq = 1.0 / (ROPE_THETA ** (jnp.arange(half, dtype=jnp.float32) * (2.0 / head_dim)))
-        freq = jnp.concatenate([inv_freq, inv_freq])[None, :]
+        inv_freq = 1.0 / (ROPE_THETA ** (np.arange(head_dim // 2) * (2.0 / head_dim)))
+        freq = jnp.asarray(np.concatenate([inv_freq, inv_freq])[None, :], jnp.float32)
         pages = (blocks * page_size * heads, head_dim)
         attended, k_out, v_out = attention(
             flat, tree_mask, depth, ctx_len, block_table, freq, k_cache.reshape(pages), v_cache.reshape(pages),

time: 129 us -> 123 us (0.953)
  Pallas kernels: 126 us -> 121 us
    pallas_call x1, Pallas kernels: 103 us -> 99.4 us  [tail(): pl.pallas_call(functools.partial(tail_kernel, chips), name='tail', out_sh...]
    pallas_call x1, Pallas kernels: 23.5 us -> 21.8 us  [attention(): pl.pallas_call(functools.partial(attention_kernel, dims), name='attend',...]
where the time goes in v1:
time: 123 us
  Pallas kernels  121 us (98%)
  other arithmetic  1.34 us (1%)
    pallas_call x1, Pallas kernels, tail(): pl.pallas_call(functools.partial(tail_kernel, chips), name='tail', out_sh...  99.4 us
    pallas_call x1, Pallas kernels, attention(): pl.pallas_call(functools.partial(attention_kernel, dims), name='attend',...  21.8 us

profile of v1, /device:TPU:113, one launch (start us, length us, event | category | flops | bytes accessed | tf_op | source)
XLA Modules:
  0.0 123.2 jit_solution(16759442689340240225)
XLA Ops:
  0.6 21.8 %attend.1 = (bf16[384,512]{1,0:T(8,128)(2,1)}, bf16[12288,128]{1,0:T(8,128)(2,1)}, bf16[12288,128]{1,0:T(8,128)(2,1)}) custom-call(s32[16]{0:T(128)} %ctx_ref.1, s32[16,12]{1,0:T(8,128)} %table_ref.1, s32[16,24]{1,0:T(8,128)} %depth_ref.1, f32[1,128]{1,0:T(1,128)} %constant.2.clone.freq_ref, bf16[384,4096]{1,0:T(8,128)(2,1)} %bitcast.12, ...), custom_call_target="tpu_custom_call" | custom-call | tf_op jit(solution)/shard_map/attend/pallas_call | solution.py:221
  22.5 99.4 %tail.1 = (f32[16,24]{1,0:T(8,128)}, f32[16,24]{1,0:T(8,128)}, f32[16,24]{1,0:T(8,128)}) custom-call(bf16[384,512]{1,0:T(8,128)(2,1)} %get-tuple-element.10.att_ref, bf16[384,4096]{1,0:T(8,128)(2,1)} %bitcast.13, bf16[32,128]{1,0:T(8,128)(2,1)} %bitcast.19, bf16[32,128]{1,0:T(8,128)(2,1)} %bitcast.20, s32[16,24]{1,0:T(8,128)} %score_ref.1, ...), custom_call_target="tpu_custom_call" | custom-call | tf_op jit(solution)/shard_map/tail/pallas_call | solution.py:641
  121.8 1.3 %fusion = (f32[16,24]{1,0:T(8,128)}, f32[16,24]{1,0:T(8,128)}) fusion(f32[16,24]{1,0:T(8,128)} %get-tuple-element.13, f32[16,24]{1,0:T(8,128)} %get-tuple-element.11, f32[16,24]{1,0:T(8,128)} %get-tuple-element.12), kind=kLoop, calls=%fused_computation.1 | loop fusion | flops 768 | bytes 7680 | tf_op jit(solution)/shard_map/sub | solution.py:673

commit v2 on v1

--- a/solution.py
+++ b/solution.py
@@ -14,7 +14,7 @@
 SPAN = 1024
 GATE = 512
 HEAD = 1024
-TILE = 256
+TILE = 512
 VMEM_LIMIT = 66_000_000
 HBM = pl.BlockSpec(memory_space=pl.ANY)
 VMEM = pl.BlockSpec(memory_space=pltpu.VMEM)
@@ -381,15 +381,13 @@
 
         lax.fori_loop(0, STEPS, one, 0)
 
-    def reduce(phase, lhs_ref, w_ref, before, filler):
+    def reduce_start(phase, lhs_ref, w_ref, before):
         def step(c, _):
-            @pl.when(c < STEPS)
-            def _():
-                before(c)
-                part[:, cols(c)] = jnp.dot(lhs_ref[...], w_ref[:, cols(c)], preferred_element_type=f32).astype(bf16)
-                plan(phase, c, "pair").start()
-
-            @pl.when((c >= 1) & (c <= STEPS))
+            before(c)
+            part[:, cols(c)] = jnp.dot(lhs_ref[...], w_ref[:, cols(c)], preferred_element_type=f32).astype(bf16)
+            plan(phase, c, "pair").start()
+
+            @pl.when(c >= 1)
             def _():
                 pair_sum(phase, c - 1)
 
@@ -399,11 +397,22 @@
 
             return 0
 
-        lax.fori_loop(0, STEPS + 3, step, 0)
+        lax.fori_loop(0, STEPS, step, 0)
+
+    def reduce_end(phase, filler):
+        def step(c, _):
+            @pl.when(c <= STEPS)
+            def _():
+                pair_sum(phase, c - 1)
+
+            accumulate(phase, c - 3)
+            return 0
+
+        lax.fori_loop(STEPS, STEPS + 3, step, 0)
         filler()
         finish(phase)
 
-    def gather(phase, compute, loads):
+    def gather(phase, compute, loads, early):
         forward(phase, 0)
         forward(phase, 1)
         share(phase, 0)
@@ -414,7 +423,10 @@
 
         def step(c, _):
             compute(cols(c), False, 0)
-            share(phase, c + 1)
+
+            @pl.when(c <= 1)
+            def _():
+                share(phase, c + 1)
 
             @pl.when(c == 0)
             def _():
@@ -426,16 +438,16 @@
             def _():
                 share(phase, 3)
 
-            @pl.when(c == 0)
-            def _():
-                ready(phase, 1)
-
-            return 0
-
-        lax.fori_loop(0, 2, step, 0)
-        ready(phase, 2)
-        ready(phase, 3)
-        compute(pl.ds(2 * wide, 2 * wide), True, None)
+            @pl.when(c + 1 < early)
+            def _():
+                ready(phase, c + 1)
+
+            return 0
+
+        lax.fori_loop(0, early, step, 0)
+        for c in range(early, STEPS):
+            ready(phase, c)
+        compute(pl.ds(early * wide, (STEPS - early) * wide), True, None)
 
     def layer(wo, wg, wu, wd, gate_acc, up_acc):
         loads = [
@@ -466,7 +478,8 @@
             own_rows.wait()
 
         pl.semaphore_wait(barrier, members - 1)
-        reduce(0, att_ref, wo, before, filler)
+        reduce_start(0, att_ref, wo, before)
+        reduce_end(0, filler)
 
         def gated(span, is_last, half):
             def close(start, width):
@@ -496,10 +509,10 @@
             else:
                 tile(full * GATE, ffn - full * GATE)
 
-        gather(0, gated, loads[:2])
+        gather(0, gated, loads[:2], STEPS - 1)
         drain(0)
         loads[2].wait()
-        reduce(1, act, wd, lambda c: None, lambda: None)
+        reduce_start(1, act, wd, lambda c: None)
 
     pl.run_scoped(
         layer,
@@ -524,7 +537,6 @@
             want_ref[pl.ds(pl.multiple_of(b * nodes, 8), nodes), :] = jnp.broadcast_to(column, (nodes, 128))
             return 0
 
-        lax.fori_loop(0, score_ref.shape[0], want_step, 0)
         run_max[...] = jnp.full(run_max.shape, -jnp.inf, f32)
         run_sum[...] = jnp.zeros(run_sum.shape, f32)
         run_pick[...] = jnp.zeros(run_pick.shape, f32)
@@ -570,8 +582,12 @@
                 lax.fori_loop(cut, full, step, 0)
                 tile(full * HEAD, rest)
 
-        acc[...] = jnp.zeros(acc.shape, f32)
-        gather(1, logits, loads)
+        def filler():
+            lax.fori_loop(0, score_ref.shape[0], want_step, 0)
+            acc[...] = jnp.zeros(acc.shape, f32)
+
+        reduce_end(1, filler)
+        gather(1, logits, loads, STEPS - 2)
         fold(full * HEAD, whole)
         end = acc[:, full * HEAD + whole:vocab]
         top = jnp.maximum(jnp.max(run_max[...], axis=-1, keepdims=True), jnp.max(end, axis=-1, keepdims=True))

time: 123 us -> 121 us (0.984)
  Pallas kernels: 121 us -> 119 us
    pallas_call x1, Pallas kernels: 99.4 us -> 97.9 us  [tail(): pl.pallas_call(functools.partial(tail_kernel, chips), name='tail', out_sh...]
where the time goes in v2:
time: 121 us
  Pallas kernels  119 us (98%)
  other arithmetic  1.34 us (1%)
    pallas_call x1, Pallas kernels, tail(): pl.pallas_call(functools.partial(tail_kernel, chips), name='tail', out_sh...  97.9 us
    pallas_call x1, Pallas kernels, attention(): pl.pallas_call(functools.partial(attention_kernel, dims), name='attend',...  21.4 us

profile of v2, /device:TPU:113, one launch (start us, length us, event | category | flops | bytes accessed | tf_op | source)
XLA Modules:
  0.0 121.3 jit_solution(2371076293531610158)
XLA Ops:
  0.6 21.4 %attend.1 = (bf16[384,512]{1,0:T(8,128)(2,1)}, bf16[12288,128]{1,0:T(8,128)(2,1)}, bf16[12288,128]{1,0:T(8,128)(2,1)}) custom-call(s32[16]{0:T(128)} %ctx_ref.1, s32[16,12]{1,0:T(8,128)} %table_ref.1, s32[16,24]{1,0:T(8,128)} %depth_ref.1, f32[1,128]{1,0:T(1,128)} %constant.2.clone.freq_ref, bf16[384,4096]{1,0:T(8,128)(2,1)} %bitcast.12, ...), custom_call_target="tpu_custom_call" | custom-call | tf_op jit(solution)/shard_map/attend/pallas_call | solution.py:221
  22.0 97.9 %tail.1 = (f32[16,24]{1,0:T(8,128)}, f32[16,24]{1,0:T(8,128)}, f32[16,24]{1,0:T(8,128)}) custom-call(bf16[384,512]{1,0:T(8,128)(2,1)} %get-tuple-element.10.att_ref, bf16[384,4096]{1,0:T(8,128)(2,1)} %bitcast.13, bf16[32,128]{1,0:T(8,128)(2,1)} %bitcast.19, bf16[32,128]{1,0:T(8,128)(2,1)} %bitcast.20, s32[16,24]{1,0:T(8,128)} %score_ref.1, ...), custom_call_target="tpu_custom_call" | custom-call | tf_op jit(solution)/shard_map/tail/pallas_call | solution.py:657
  120.0 1.3 %fusion = (f32[16,24]{1,0:T(8,128)}, f32[16,24]{1,0:T(8,128)}) fusion(f32[16,24]{1,0:T(8,128)} %get-tuple-element.13, f32[16,24]{1,0:T(8,128)} %get-tuple-element.11, f32[16,24]{1,0:T(8,128)} %get-tuple-element.12), kind=kLoop, calls=%fused_computation.1 | loop fusion | flops 768 | bytes 7680 | tf_op jit(solution)/shard_map/sub | solution.py:689

commit v3 on v2

--- a/solution.py
+++ b/solution.py
@@ -45,8 +45,8 @@
 
 
 def attention_kernel(
-    dims, ctx_ref, table_ref, depth_ref, freq_ref, hidden_hbm, gain_ref, mask_ref, wq_hbm, wk_hbm, wv_hbm, k_hbm, v_hbm,
-    att_ref, k_out, v_out, hid, normed, weights, kc, vc, cosine, sine, gain_buf, head_bias, q_buf, k_buf, v_buf, o_buf, renewed, in_sems, out_sems,
+    dims, ctx_ref, table_ref, depth_hbm, freq_hbm, hidden_hbm, gain_hbm, mask_hbm, wq_hbm, wk_hbm, wv_hbm, k_hbm, v_hbm,
+    att_out, k_out, v_out, depth_ref, freq_ref, gain_ref, mask_ref, att_ref, hid, normed, weights, kc, vc, cosine, sine, gain_buf, head_bias, q_buf, k_buf, v_buf, o_buf, renewed, in_sems, out_sems, small_sems,
 ):
     requests, nodes, pages, page_rows, heads, head_dim = dims
     rows = requests * nodes
@@ -62,21 +62,31 @@
         copies.append(pltpu.make_async_copy(w, weights.at[i], in_sems.at[2 + i]))
     copies.append(pltpu.make_async_copy(k_hbm, kc, in_sems.at[5]))
     copies.append(pltpu.make_async_copy(v_hbm, vc, in_sems.at[6]))
-    for copy in copies[:3]:
+    small = [
+        pltpu.make_async_copy(src, dst, small_sems.at[i])
+        for i, (src, dst) in enumerate(((gain_hbm, gain_ref), (depth_hbm, depth_ref), (freq_hbm, freq_ref), (mask_hbm, mask_ref)))
+    ]
+    for copy in small + copies[:3]:
         copy.start()
+    for copy in small:
+        copy.wait()
 
     gain_buf[...] = gain_row(gain_ref)
     lane = lax.broadcasted_iota(i32, (1, head_dim), 1)
     sign = jnp.where(lane < head_dim // 2, -1.0, 1.0)
 
-    def angle_step(b, _):
-        mine = pl.ds(pl.multiple_of(b * nodes, 8), nodes)
-        angle = (column_of(depth_ref, b) + ctx_ref[b].astype(f32)) * freq_ref[...]
-        cosine[mine, :] = jnp.cos(angle)
-        sine[mine, :] = jnp.sin(angle) * sign
+    together = 4
+
+    def angle_step(i, _):
+        for k in range(together):
+            b = i * together + k
+            mine = pl.ds(pl.multiple_of(b * nodes, 8), nodes)
+            angle = (column_of(depth_ref, b) + ctx_ref[b].astype(f32)) * freq_ref[...]
+            cosine[mine, :] = jnp.cos(angle)
+            sine[mine, :] = jnp.sin(angle) * sign
         return 0
 
-    lax.fori_loop(0, requests, angle_step, 0)
+    lax.fori_loop(0, requests // together, angle_step, 0)
     for copy in copies[3:]:
         copy.start()
     span_col = lax.broadcasted_iota(i32, (1, span_rows), 1)
@@ -175,7 +185,6 @@
                 stores.append((c, j, page, jnp.where(fresh[piece], fill, old).astype(bf16)))
         return mine, mixed, stores
 
-    together = 4
     for whole in flush:
         whole.wait()
 
@@ -196,8 +205,11 @@
 
     lax.fori_loop(0, requests // together, request_step, 0)
     att_ref[...] = o_buf[...].astype(bf16)
+    att_copy = pltpu.make_async_copy(att_ref, att_out, small_sems.at[4])
+    att_copy.start()
     for c, out in enumerate((k_out, v_out)):
         pltpu.make_async_copy(renewed.at[c], out.at[pl.ds(0, requests * window), :], out_sems.at[2 + c]).wait()
+    att_copy.wait()
 
 
 def attention(hidden, tree_mask, depth, ctx_len, block_table, freq, k_pages, v_pages, attn_norm, w_q, w_k, w_v, dims):
@@ -208,6 +220,11 @@
     bf16, f32 = jnp.bfloat16, jnp.float32
     window = window_pages(nodes, page_rows // heads) * page_rows
     scratch = [
+        pltpu.VMEM(depth.shape, jnp.int32),
+        pltpu.VMEM(freq.shape, f32),
+        pltpu.VMEM(attn_norm.shape, bf16),
+        pltpu.VMEM(tree_mask.shape, jnp.int32),
+        pltpu.VMEM((rows, width), bf16),
         pltpu.VMEM((rows, model), bf16),
         pltpu.VMEM((rows, model), bf16),
         pltpu.VMEM((3, model, width), bf16),
@@ -217,7 +234,7 @@
         pltpu.VMEM((rows, head_dim), f32),
         pltpu.VMEM((1, model), f32),
         pltpu.VMEM((heads * nodes, pages * page_rows), f32),
-    ] + [pltpu.VMEM((rows, width), f32)] * 4 + [pltpu.VMEM((2, requests * window, head_dim), bf16), pltpu.SemaphoreType.DMA((7,)), pltpu.SemaphoreType.DMA((4,))]
+    ] + [pltpu.VMEM((rows, width), f32)] * 4 + [pltpu.VMEM((2, requests * window, head_dim), bf16), pltpu.SemaphoreType.DMA((7,)), pltpu.SemaphoreType.DMA((4,)), pltpu.SemaphoreType.DMA((5,))]
     return pl.pallas_call(
         functools.partial(attention_kernel, dims),
         name="attend",
@@ -226,17 +243,17 @@
             jax.ShapeDtypeStruct(k_pages.shape, bf16),
             jax.ShapeDtypeStruct(v_pages.shape, bf16),
         ),
-        in_specs=[SMEM, SMEM, VMEM, VMEM, HBM, VMEM, VMEM, HBM, HBM, HBM, HBM, HBM],
-        out_specs=(VMEM, HBM, HBM),
+        in_specs=[SMEM, SMEM] + [HBM] * 10,
+        out_specs=(HBM, HBM, HBM),
         scratch_shapes=scratch,
         compiler_params=pltpu.CompilerParams(vmem_limit_bytes=VMEM_LIMIT),
     )(ctx_len, block_table, depth, freq, hidden, attn_norm, tree_mask, w_q, w_k, w_v, k_pages, v_pages)
 
 
 def tail_kernel(
-    chips, att_ref, hid_hbm, mlp_gain_ref, fin_gain_ref, score_ref, wo_hbm, wg_hbm, wu_hbm, wd_hbm, lm_hbm,
-    top_ref, total_ref, pick_ref, part, sib_in, rel_l, rel_r, in_l, in_r, xg, act, hid_own, run_max, run_sum, run_pick, stats, want_ref, gains,
-    send_sems, recv_sems, stat_send, stat_recv, w_sems, wo_sems, lm_sems, hid_sem,
+    chips, att_hbm, hid_hbm, mlp_gain_hbm, fin_gain_hbm, score_hbm, wo_hbm, wg_hbm, wu_hbm, wd_hbm, lm_hbm,
+    top_ref, total_ref, pick_ref, att_ref, mlp_gain_ref, fin_gain_ref, score_ref, part, sib_in, rel_l, rel_r, in_l, in_r, xg, act, hid_own, run_max, run_sum, run_pick, stats, want_ref, gains,
+    send_sems, recv_sems, stat_send, stat_recv, w_sems, wo_sems, lm_sems, hid_sem, small_sems,
 ):
     f32, bf16 = jnp.float32, jnp.bfloat16
     rows, model = xg.shape
@@ -457,8 +474,17 @@
         def wo_piece(c):
             return pltpu.make_async_copy(wo_hbm.at[:, cols(c)], wo.at[:, cols(c)], wo_sems.at[c])
 
+        small = [
+            pltpu.make_async_copy(src, dst, small_sems.at[i])
+            for i, (src, dst) in enumerate((
+                (att_hbm, att_ref), (mlp_gain_hbm, mlp_gain_ref), (fin_gain_hbm, fin_gain_ref), (score_hbm, score_ref),
+            ))
+        ]
+        small[0].start()
         for c in steps:
             wo_piece(c).start()
+        for copy in small[1:]:
+            copy.start()
         own_rows = pltpu.make_async_copy(hid_hbm.at[block(0), :], hid_own, hid_sem.at[0])
         own_rows.start()
 
@@ -471,12 +497,15 @@
                     load.start()
 
         def filler():
+            for copy in small[1:]:
+                copy.wait()
             gains[0:1, :] = gain_row(mlp_gain_ref)
             gains[1:2, :] = gain_row(fin_gain_ref)
             gate_acc[...] = jnp.zeros(gate_acc.shape, f32)
             up_acc[...] = jnp.zeros(up_acc.shape, f32)
             own_rows.wait()
 
+        small[0].wait()
         pl.semaphore_wait(barrier, members - 1)
         reduce_start(0, att_ref, wo, before)
         reduce_end(0, filler)
@@ -630,6 +659,10 @@
     bf16, f32 = jnp.bfloat16, jnp.float32
     own = rows // members
     scratch = [
+        pltpu.VMEM(attended.shape, bf16),
+        pltpu.VMEM(mlp_norm.shape, bf16),
+        pltpu.VMEM(final_norm.shape, bf16),
+        pltpu.VMEM(score_id.shape, jnp.int32),
         pltpu.VMEM((rows, model), bf16),
         pltpu.VMEM((rows // 2, model), bf16),
         pltpu.VMEM((own, model // 2), bf16),
@@ -653,12 +686,13 @@
         pltpu.SemaphoreType.DMA((STEPS,)),
         pltpu.SemaphoreType.DMA((5,)),
         pltpu.SemaphoreType.DMA((1,)),
+        pltpu.SemaphoreType.DMA((4,)),
     ]
     return pl.pallas_call(
         functools.partial(tail_kernel, chips),
         name="tail",
         out_shape=(jax.ShapeDtypeStruct(score_id.shape, f32),) * 3,
-        in_specs=[VMEM, HBM, VMEM, VMEM, VMEM, HBM, HBM, HBM, HBM, HBM],
+        in_specs=[HBM] * 10,
         out_specs=(VMEM, VMEM, VMEM),
         scratch_shapes=scratch,
         compiler_params=pltpu.CompilerParams(vmem_limit_bytes=VMEM_LIMIT, collective_id=0, has_side_effects=True),

time: 121 us -> 121 us (level)
  no operation moved by 1% of the time
where the time goes in v3:
time: 121 us
  Pallas kernels  119 us (98%)
  other arithmetic  1.34 us (1%)
    pallas_call x1, Pallas kernels, tail(): pl.pallas_call(functools.partial(tail_kernel, chips), name='tail', out_sh...  97.1 us
    pallas_call x1, Pallas kernels, attention(): pl.pallas_call(functools.partial(attention_kernel, dims), name='attend',...  21.5 us

profile of v3, /device:TPU:113, one launch (start us, length us, event | category | flops | bytes accessed | tf_op | source)
XLA Modules:
  0.0 120.5 jit_solution(7853662717916185422)
XLA Ops:
  0.6 21.5 %attend.1 = (bf16[384,512]{1,0:T(8,128)(2,1)}, bf16[12288,128]{1,0:T(8,128)(2,1)}, bf16[12288,128]{1,0:T(8,128)(2,1)}) custom-call(s32[16]{0:T(128)} %ctx_ref.1, s32[16,12]{1,0:T(8,128)} %table_ref.1, s32[16,24]{1,0:T(8,128)} %depth_hbm.1, f32[1,128]{1,0:T(1,128)} %constant.2.clone.freq_hbm, bf16[384,4096]{1,0:T(8,128)(2,1)} %bitcast.12, ...), custom_call_target="tpu_custom_call" | custom-call | tf_op jit(solution)/shard_map/attend/pallas_call | solution.py:238
  22.1 97.1 %tail.1 = (f32[16,24]{1,0:T(8,128)}, f32[16,24]{1,0:T(8,128)}, f32[16,24]{1,0:T(8,128)}) custom-call(bf16[384,512]{1,0:T(8,128)(2,1)} %get-tuple-element.10.att_hbm, bf16[384,4096]{1,0:T(8,128)(2,1)} %bitcast.13, bf16[32,128]{1,0:T(8,128)(2,1)} %bitcast.19, bf16[32,128]{1,0:T(8,128)(2,1)} %bitcast.20, s32[16,24]{1,0:T(8,128)} %score_hbm.1, ...), custom_call_target="tpu_custom_call" | custom-call | tf_op jit(solution)/shard_map/tail/pallas_call | solution.py:691
  119.2 1.3 %fusion = (f32[16,24]{1,0:T(8,128)}, f32[16,24]{1,0:T(8,128)}) fusion(f32[16,24]{1,0:T(8,128)} %get-tuple-element.13, f32[16,24]{1,0:T(8,128)} %get-tuple-element.11, f32[16,24]{1,0:T(8,128)} %get-tuple-element.12), kind=kLoop, calls=%fused_computation.1 | loop fusion | flops 768 | bytes 7680 | tf_op jit(solution)/shard_map/sub | solution.py:723

commit v4 on v3

--- a/solution.py
+++ b/solution.py
@@ -66,10 +66,11 @@
         pltpu.make_async_copy(src, dst, small_sems.at[i])
         for i, (src, dst) in enumerate(((gain_hbm, gain_ref), (depth_hbm, depth_ref), (freq_hbm, freq_ref), (mask_hbm, mask_ref)))
     ]
-    for copy in small + copies[:3]:
+    for copy in small + copies[:2]:
         copy.start()
     for copy in small:
         copy.wait()
+    copies[2].start()
 
     gain_buf[...] = gain_row(gain_ref)
     lane = lax.broadcasted_iota(i32, (1, head_dim), 1)
@@ -87,8 +88,6 @@
         return 0
 
     lax.fori_loop(0, requests // together, angle_step, 0)
-    for copy in copies[3:]:
-        copy.start()
     span_col = lax.broadcasted_iota(i32, (1, span_rows), 1)
     slot_col = span_col // heads
     stack_row = lax.broadcasted_iota(i32, (stack, 1), 0)
@@ -111,6 +110,7 @@
             return 0
 
         lax.fori_loop(0, half_rows // group // 2, norm_step, 0)
+        copies[3 + part].start()
 
     flush = [pltpu.make_async_copy(cache, out, out_sems.at[k]) for k, (cache, out) in enumerate(((kc, k_out), (vc, v_out)))]
     width = heads * head_dim
@@ -130,10 +130,12 @@
             return 0
 
         lax.fori_loop(0, width // TILE, project, 0)
-        if i == 1:
-            for k, whole in enumerate(flush):
-                copies[5 + k].wait()
-                whole.start()
+        if i == 0:
+            copies[5].start()
+            copies[6].start()
+    for k, whole in enumerate(flush):
+        copies[5 + k].wait()
+        whole.start()
 
     touched = window_pages(nodes, page_rows // heads)
     window = touched * page_rows
@@ -185,8 +187,6 @@
                 stores.append((c, j, page, jnp.where(fresh[piece], fill, old).astype(bf16)))
         return mine, mixed, stores
 
-    for whole in flush:
-        whole.wait()
 
     def request_step(i, _):
         done = [attend(i * together + k) for k in range(together)]
@@ -196,6 +196,12 @@
             for c, j, page, value in stores:
                 slot = pl.ds(pl.multiple_of((i * together + k) * window + j * page_rows, page_rows), page_rows)
                 renewed[c, slot, :] = value
+
+        @pl.when(i == 0)
+        def _():
+            for whole in flush:
+                whole.wait()
+
         for k, (mine, mixed, stores) in enumerate(done):
             for c, j, page, value in stores:
                 slot = pl.ds(pl.multiple_of((i * together + k) * window + j * page_rows, page_rows), page_rows)

time: 121 us -> 120 us (level)
  no operation moved by 1% of the time
where the time goes in v4:
time: 120 us
  Pallas kernels  118 us (98%)
  other arithmetic  1.34 us (1%)
    pallas_call x1, Pallas kernels, tail(): pl.pallas_call(functools.partial(tail_kernel, chips), name='tail', out_sh...  97 us
    pallas_call x1, Pallas kernels, attention(): pl.pallas_call(functools.partial(attention_kernel, dims), name='attend',...  21 us

profile of v4, /device:TPU:113, one launch (start us, length us, event | category | flops | bytes accessed | tf_op | source)
XLA Modules:
  0.0 120.0 jit_solution(18405154202737023677)
XLA Ops:
  0.6 21.0 %attend.1 = (bf16[384,512]{1,0:T(8,128)(2,1)}, bf16[12288,128]{1,0:T(8,128)(2,1)}, bf16[12288,128]{1,0:T(8,128)(2,1)}) custom-call(s32[16]{0:T(128)} %ctx_ref.1, s32[16,12]{1,0:T(8,128)} %table_ref.1, s32[16,24]{1,0:T(8,128)} %depth_hbm.1, f32[1,128]{1,0:T(1,128)} %constant.2.clone.freq_hbm, bf16[384,4096]{1,0:T(8,128)(2,1)} %bitcast.12, ...), custom_call_target="tpu_custom_call" | custom-call | tf_op jit(solution)/shard_map/attend/pallas_call | solution.py:244
  21.6 97.0 %tail.1 = (f32[16,24]{1,0:T(8,128)}, f32[16,24]{1,0:T(8,128)}, f32[16,24]{1,0:T(8,128)}) custom-call(bf16[384,512]{1,0:T(8,128)(2,1)} %get-tuple-element.10.att_hbm, bf16[384,4096]{1,0:T(8,128)(2,1)} %bitcast.13, bf16[32,128]{1,0:T(8,128)(2,1)} %bitcast.19, bf16[32,128]{1,0:T(8,128)(2,1)} %bitcast.20, s32[16,24]{1,0:T(8,128)} %score_hbm.1, ...), custom_call_target="tpu_custom_call" | custom-call | tf_op jit(solution)/shard_map/tail/pallas_call | solution.py:697
  118.7 1.3 %fusion = (f32[16,24]{1,0:T(8,128)}, f32[16,24]{1,0:T(8,128)}) fusion(f32[16,24]{1,0:T(8,128)} %get-tuple-element.13, f32[16,24]{1,0:T(8,128)} %get-tuple-element.11, f32[16,24]{1,0:T(8,128)} %get-tuple-element.12), kind=kLoop, calls=%fused_computation.1 | loop fusion | flops 768 | bytes 7680 | tf_op jit(solution)/shard_map/sub | solution.py:729
